TPU v7x, 32 devices: a whole 2x2x4 slice. The times are simulated.
32 devices in a mesh: group: 8 (over y, x, core), tile: 4 (over z).
Axes of the slice: x: 2, y: 2, z: 4, core: 2. Of those that a mesh axis runs over, the one named last changes fastest.
Arguments:
- coupling: float32 [32, 1024, 768], P('group', None, 'tile'), may hold values from -6 to 6
- interior_solve: float32 [32, 768, 1024], P('group', 'tile'), may hold values from -0.21875 to 0.21875
- boundary_stiffness: float32 [32, 1024, 1024], P('group', 'tile'), may hold values from -6 to 6
- migration: int32 [32], replicated, may hold values from -1 to 15, as said below
Outputs:
- condensed: float32 [16, 1024, 1024], P('group', 'tile')
Inputs may be any that keep to these rules, and one draw needn't show every extreme that they name: `migration`: every condensed slot is named by exactly one RVE slot; RVE slots of group g are g * 4 to g * 4 + 3; the condensed slots of group g are named only by RVE slots of group g or of its partner, the group whose index differs from g in the lowest bit; some group holds 4 plastic RVEs.
All inputs are finite; a program needn't handle non-finite values.
Results may differ from a plain program's by a relative error of at most 0.000071.
Values sent between devices are 32-bit elements; how exact they have to be, the bound alone decides.
A program may use at most 64 MiB of HBM per device.

v0:
```python
import jax
import jax.numpy as jnp
from jax import lax
from jax.sharding import PartitionSpec as P

OWN = 2


def swapped(array, axis, distance):
    return lax.ppermute(array, axis, [(i, i ^ 1 << distance) for i in range(lax.axis_size(axis))])


def condense(coupling_cols, solve_rows, stiff_rows):
    product = lax.psum_scatter(
        jnp.dot(
            coupling_cols,
            solve_rows,
            precision=lax.Precision.HIGHEST,
            preferred_element_type=jnp.float32,
        ),
        "tile",
        scatter_dimension=0,
        tiled=True,
    )
    return stiff_rows - product


def select_slots(stacked, positions, present):
    chosen = jnp.take(stacked, positions, axis=0)
    shaped = present.reshape((-1,) + (1,) * (stacked.ndim - 1))
    return jnp.where(shaped, chosen, jnp.zeros_like(chosen))


def body(coupling, interior_solve, boundary_stiffness, migration):
    home_count = coupling.shape[0]
    mygroup = lax.axis_index("group")
    partner = jnp.bitwise_xor(mygroup, 1)
    own_plan = lax.dynamic_slice_in_dim(migration, mygroup * home_count, home_count)
    slot_ids = jnp.arange(OWN, dtype=jnp.int32)
    local_ids = jnp.arange(home_count, dtype=jnp.int32)

    def locate(wanted):
        matches = own_plan[None, :] == wanted[:, None]
        positions = jnp.sum(jnp.where(matches, local_ids[None, :], 0), axis=1)
        return (positions, jnp.any(matches, axis=1))

    mine_index, mine_here = locate(mygroup * OWN + slot_ids)
    their_index, their_here = locate(partner * OWN + slot_ids)
    keep_mask = mine_here[:, None, None]
    outgoing = (
        select_slots(coupling, their_index, their_here),
        select_slots(interior_solve, their_index, their_here),
        select_slots(boundary_stiffness, their_index, their_here),
    )
    arrived = swapped((outgoing[0], outgoing[1], outgoing[2]), "group", 0)
    kept_coupling = jnp.where(keep_mask, jnp.take(coupling, mine_index, axis=0), arrived[0])
    kept_solve = jnp.where(keep_mask, jnp.take(interior_solve, mine_index, axis=0), arrived[1])
    kept_stiff = jnp.where(keep_mask, jnp.take(boundary_stiffness, mine_index, axis=0), arrived[2])
    result = jnp.stack(
        [condense(kept_coupling[slot], kept_solve[slot], kept_stiff[slot]) for slot in range(OWN)]
    )
    return result


def solution(mesh):
    return jax.shard_map(
        body,
        mesh=mesh,
        in_specs=(
            P("group", None, "tile"),
            P("group", "tile", None),
            P("group", "tile", None),
            P(),
        ),
        out_specs=P("group", "tile", None),
        check_vma=False,
    )
```

profile of v0, /device:TPU:8, one launch (start us, length us, event | category | flops | bytes accessed | tf_op | source)
XLA Modules:
  0.0 205.4 jit_solution(3017204221030186767)
XLA Ops:
  6.5 0.9 dynamic_slice.3
  7.4 0.2 fusion.6
  7.7 0.2 compare_reduce_fusion.1
  7.9 0.6 copy-done
  8.4 1.8 gather_fusion.3
  10.2 2.9 %select_select_fusion.4 = f32[2,1024,192]{1,2,0:T(8,128)} fusion(f32[2,1024,192]{1,2,0:T(8,128)} %gather_fusion.3, pred[2]{0:T(512)(128)(4,1)S(1)} %compare_and_fusion, pred[2]{0:T(512)(128)(4,1)S(1)} %get-tuple-element.8), kind=kLoop, calls=%fused_computation.11 | loop fusion | flops 786432 | bytes 3145732 | tf_op jit(solution)/shard_map/jit(_where)/select_n | solution.py:31
  13.1 3.7 %gather_fusion.5 = f32[2,192,1024]{2,1,0:T(8,128)} fusion(f32[4,192,1024]{2,1,0:T(8,128)} %param.11, s32[1024]{0:T(1024)S(1)} %pad_clamp_fusion), kind=kCustom, calls=%fused_computation.5.clone | custom fusion | bytes 3145736 | tf_op jit(solution)/shard_map/jit(_take)/gather | solution.py:29
  16.8 2.9 %select_select_fusion.2 = f32[2,192,1024]{2,1,0:T(8,128)} fusion(f32[2,192,1024]{2,1,0:T(8,128)} %gather_fusion.5, pred[2]{0:T(512)(128)(4,1)S(1)} %compare_and_fusion, pred[2]{0:T(512)(128)(4,1)S(1)} %get-tuple-element.8), kind=kLoop, calls=%fused_computation.9 | loop fusion | flops 786432 | bytes 3145732 | tf_op jit(solution)/shard_map/jit(_where)/select_n | solution.py:31
  19.7 0.5 collective-permute-start.2
  20.2 1.8 gather_fusion.2
  22.0 3.7 %gather_fusion.4 = f32[2,192,1024]{2,1,0:T(8,128)} fusion(f32[4,192,1024]{2,1,0:T(8,128)} %param.11, s32[1024]{0:T(1024)S(1)} %pad_clamp_fusion.1), kind=kCustom, calls=%fused_computation.2.clone | custom fusion | bytes 3145736 | tf_op jit(solution)/shard_map/jit(_take)/gather | solution.py:57
  25.7 2.3 %select_select_fusion.5 = f32[2,1024,192]{1,2,0:T(8,128)S(1)} fusion(f32[2,1024,192]{1,2,0:T(8,128)} %collective-permute-done.1, f32[2,1024,192]{1,2,0:T(8,128)} %gather_fusion.2, pred[2]{0:T(512)(128)(4,1)S(1)} %compare_and_fusion.1, pred[2]{0:T(512)(128)(4,1)S(1)} %get-tuple-element.6), kind=kLoop, calls=%fused_computation.12 | loop fusion | flops 786432 | bytes 4718596 | tf_op jit(solution)/shard_map/jit(_where)/select_n | solution.py:56
  28.1 2.3 %select_select_fusion.3 = f32[2,192,1024]{2,1,0:T(8,128)S(1)} fusion(f32[2,192,1024]{2,1,0:T(8,128)} %collective-permute-done.2, f32[2,192,1024]{2,1,0:T(8,128)S(1)} %copy-done.1, pred[2]{0:T(512)(128)(4,1)S(1)} %compare_and_fusion.1, pred[2]{0:T(512)(128)(4,1)S(1)} %get-tuple-element.6), kind=kLoop, calls=%fused_computation.10 | loop fusion | flops 786432 | bytes 4718596 | tf_op jit(solution)/shard_map/jit(_where)/select_n | solution.py:57
  30.4 1.1 copy-done.3
  31.6 5.2 %fusion.4 = f32[1024,1024]{1,0:T(8,128)} fusion(f32[2,192,1024]{2,1,0:T(8,128)S(1)} %select_select_fusion.3, f32[2,1024,192]{1,2,0:T(8,128)S(1)} %select_select_fusion.5), kind=kOutput, calls=%fused_computation.20 | convolution fusion | flops 2415919104 | bytes 5767168 | tf_op jit(solution)/shard_map/dot_general | solution.py:15
  36.9 6.8 %fusion.5 = f32[1024,1024]{1,0:T(8,128)} fusion(f32[2,192,1024]{2,1,0:T(8,128)} %copy-done.3, f32[2,1024,192]{1,2,0:T(8,128)} %copy-done.2), kind=kOutput, calls=%fused_computation.23 | convolution fusion | flops 2415919104 | bytes 5767168 | tf_op jit(solution)/shard_map/dot_general | solution.py:15
  43.7 4.9 %gather_fusion.1 = f32[2,256,1024]{2,1,0:T(8,128)} fusion(f32[4,256,1024]{2,1,0:T(8,128)} %param.12, s32[1024]{0:T(1024)S(1)} %pad_clamp_fusion), kind=kCustom, calls=%fused_computation.3.clone | custom fusion | bytes 4194312 | tf_op jit(solution)/shard_map/jit(_take)/gather | solution.py:29
  48.6 3.4 %select_select_fusion = f32[2,256,1024]{2,1,0:T(8,128)} fusion(f32[2,256,1024]{2,1,0:T(8,128)} %gather_fusion.1, pred[2]{0:T(512)(128)(4,1)S(1)} %compare_and_fusion, pred[2]{0:T(512)(128)(4,1)S(1)} %get-tuple-element.8), kind=kLoop, calls=%fused_computation.7 | loop fusion | flops 1048576 | bytes 4194308 | tf_op jit(solution)/shard_map/jit(_where)/select_n | solution.py:31
  52.0 4.3 %gather_fusion = f32[2,256,1024]{2,1,0:T(8,128)} fusion(f32[4,256,1024]{2,1,0:T(8,128)} %param.12, s32[1024]{0:T(1024)S(1)} %pad_clamp_fusion.1), kind=kCustom, calls=%fused_computation.clone | custom fusion | bytes 4194312 | tf_op jit(solution)/shard_map/jit(_take)/gather | solution.py:58
  56.3 0.1 collective-permute-done
  56.4 4.2 %select_select_fusion.1 = f32[2,256,1024]{2,1,0:T(8,128)} fusion(f32[2,256,1024]{2,1,0:T(8,128)} %collective-permute-done, f32[2,256,1024]{2,1,0:T(8,128)} %gather_fusion, pred[2]{0:T(512)(128)(4,1)S(1)} %compare_and_fusion.1, pred[2]{0:T(512)(128)(4,1)S(1)} %get-tuple-element.6), kind=kLoop, calls=%fused_computation.8 | loop fusion | flops 1048576 | bytes 6291460 | tf_op jit(solution)/shard_map/jit(_where)/select_n | solution.py:58
  60.7 54.2 %reduce-scatter.5.cloned.1.call-done = f32[256,1024]{1,0:T(8,128)} async-done(((f32[1024,1024]{1,0:T(8,128)}), f32[256,1024]{1,0:T(8,128)}) %reduce-scatter.5.cloned.1.call-update) | async-done | bytes 1048592 | tf_op jit(solution)/shard_map/reduce_scatter | solution.py:14
  114.9 79.6 %reduce-scatter.3.cloned.1.call-done = f32[256,1024]{1,0:T(8,128)} async-done(((f32[1024,1024]{1,0:T(8,128)}), f32[256,1024]{1,0:T(8,128)}) %reduce-scatter.3.cloned.1.call-update) | async-done | bytes 1048592 | tf_op jit(solution)/shard_map/reduce_scatter | solution.py:14
  194.5 4.0 %fusion.3 = (f32[2,256,1024]{2,1,0:T(8,128)}, f32[2,256,1024]{2,1,0:T(8,128)}) fusion(f32[256,1024]{1,0:T(8,128)} %reduce-scatter.3.cloned.1.call-done, f32[2,256,1024]{2,1,0:T(8,128)} %select_select_fusion.1, f32[256,1024]{1,0:T(8,128)} %reduce-scatter.5.cloned.1.call-done, ...), kind=kLoop, output_to_operand_aliasing={{0}: (3, {}), {1}: (3, {})}, calls=%fused_computation.18 | loop fusion | flops 524288 | bytes 6291456 | tf_op jit(solution)/shard_map/stack | solution.py:59
  (22 shorter events, 0.2 us)
Async XLA Ops:
  6.5 1.9 copy-start
  6.5 108.4 %reduce-scatter.5.cloned.1.call-start = ((), (), s32[]{:S(2)}) async-start(), calls=%async_computation.3 | async-start | bytes 5242880 | tf_op jit(solution)/shard_map/reduce_scatter | solution.py:14
  13.1 12.6 %collective-permute-start.1 = (f32[2,1024,192]{1,2,0:T(8,128)}, f32[2,1024,192]{1,2,0:T(8,128)}, u32[]{:S(2)}, u32[]{:S(2)}) collective-permute-start(f32[2,1024,192]{1,2,0:T(8,128)} %select_select_fusion.4), channel_id=1, source_target_pairs={{0,4},{4,0},{8,12},{12,8},{16,20},{20,16},{24,28},{28,24},{1,5},{5... | collective-permute-start | bytes 4718600 | tf_op jit(solution)/shard_map/ppermute | solution.py:10
  19.7 8.4 %collective-permute-start.2 = (f32[2,192,1024]{2,1,0:T(8,128)}, f32[2,192,1024]{2,1,0:T(8,128)}, u32[]{:S(2)}, u32[]{:S(2)}) collective-permute-start(f32[2,192,1024]{2,1,0:T(8,128)} %select_select_fusion.2), channel_id=1, source_target_pairs={{0,4},{4,0},{8,12},{12,8},{16,20},{20,16},{24,28},{28,24},{1,5},{5... | collective-permute-start | bytes 4718600 | tf_op jit(solution)/shard_map/ppermute | solution.py:10
  25.7 2.4 %copy-start.1 = (f32[2,192,1024]{2,1,0:T(8,128)S(1)}, f32[2,192,1024]{2,1,0:T(8,128)}, u32[]{:S(2)}) copy-start(f32[2,192,1024]{2,1,0:T(8,128)} %gather_fusion.4) | copy-start | bytes 4718596
  28.1 2.4 %copy-start.2 = (f32[2,1024,192]{1,2,0:T(8,128)}, f32[2,1024,192]{1,2,0:T(8,128)S(1)}, u32[]{:S(2)}) copy-start(f32[2,1024,192]{1,2,0:T(8,128)S(1)} %select_select_fusion.5) | copy-start | bytes 4718596
  30.4 1.1 copy-start.3
  36.8 157.7 %reduce-scatter.3.cloned.1.call-start = ((), (), s32[]{:S(2)}) async-start(), calls=%async_computation.2 | async-start | bytes 5242880 | tf_op jit(solution)/shard_map/reduce_scatter | solution.py:14
  51.9 4.5 %collective-permute-start = (f32[2,256,1024]{2,1,0:T(8,128)}, f32[2,256,1024]{2,1,0:T(8,128)}, u32[]{:S(2)}, u32[]{:S(2)}) collective-permute-start(f32[2,256,1024]{2,1,0:T(8,128)} %select_select_fusion), channel_id=1, source_target_pairs={{0,4},{4,0},{8,12},{12,8},{16,20},{20,16},{24,28},{28,24},{1,5},{5... | collective-permute-start | bytes 6291464 | tf_op jit(solution)/shard_map/ppermute | solution.py:10
Sparse Core Ops, SparseCore 0:
  36.9 77.9 reduce-scatter.4
  117.2 77.2 reduce-scatter.2
where the time goes:
time: 207 us; the launch traced here: 205 us
  waiting for transfers between devices  134 us (65%)
  local copies, waits for them, and re-layouts  22.7 us (11%)
  other arithmetic  22.6 us (11%)
  between operations  13.5 us (7%)
  matrix products  12 us (6%)
    reduce_scatter x2, waiting for transfers between devices, condense(): lax.psum_scatter(jnp.dot(coupling_cols, solve_rows, precision=lax.Precisi...  134 us
    dot_general x2, matrix products, condense(): jnp.dot(coupling_cols, solve_rows, precision=lax.Precision.HIGHEST, prefe...  12 us
    gather x3, local copies, waits for them, and re-layouts, select_slots(): chosen = jnp.take(stacked, positions, axis=0)  10.3 us
    select_n x3, other arithmetic, select_slots(): return jnp.where(shaped, chosen, jnp.zeros_like(chosen))  9.14 us
    gather x1, local copies, waits for them, and re-layouts, body(): jnp.take(boundary_stiffness, mine_index, axis=0)  4.29 us
    select_n x1, other arithmetic, body(): jnp.where(keep_mask, jnp.take(boundary_stiffness, mine_index, axis=0), ar...  4.24 us
  transfers between devices with their start and end apart: 5, of which 3 were waited for; matrix products, arithmetic and copies ran while one was open for 18% of the time, Pallas kernels for 0%

commit v1 on v0

--- a/solution.py
+++ b/solution.py
@@ -1,6 +1,8 @@
 import jax
 import jax.numpy as jnp
 from jax import lax
+from jax.experimental import pallas as pl
+from jax.experimental.pallas import tpu as pltpu
 from jax.sharding import PartitionSpec as P
 
 OWN = 2
@@ -31,7 +33,7 @@
     return jnp.where(shaped, chosen, jnp.zeros_like(chosen))
 
 
-def body(coupling, interior_solve, boundary_stiffness, migration):
+def portable_body(coupling, interior_solve, boundary_stiffness, migration):
     home_count = coupling.shape[0]
     mygroup = lax.axis_index("group")
     partner = jnp.bitwise_xor(mygroup, 1)
@@ -62,9 +64,362 @@
     return result
 
 
+MESH = pl.DeviceIdType.MESH
+LINE = 4
+CHUNKS = 4
+STRIP = 16
+
+
+def split_into(stack, slot, base, depth, rows, cols, value, order):
+    high = value.astype(jnp.bfloat16)
+    low = (value - high.astype(jnp.float32)).astype(jnp.bfloat16)
+    for place, term in enumerate(order):
+        at = pl.ds(base + place * depth + rows, value.shape[0])
+        stack[slot, at, cols] = high if term == 0 else low
+
+
+def contract(left, right):
+    return lax.dot_general(left, right, (((0,), (0,)), ((), ())), preferred_element_type=jnp.float32)
+
+
+def line_kernel(
+    plan, k_hbm, x_hbm, b_hbm, out_hbm,
+    k_home, x_home, b_home, k_out, x_out, b_out, k_in, x_in, b_in, k_got, x_got,
+    k_end, x_end, k_stack, x_stack, p_send, p_recv, e_send, e_recv, result,
+    load_sem, mig_send, mig_recv, em_send, em_recv, mm_send, mm_recv, me_send, me_recv, out_sem,
+):
+    home, depth, columns = x_home.shape
+    rows = b_home.shape[1]
+    width = columns // CHUNKS
+    last = LINE - 1
+    g, t = lax.axis_index("group"), lax.axis_index("tile")
+    partner = g + 1 - 2 * (g % 2)
+    middle = (t % last + last - 1) // last
+    is_end = middle == 0
+    is_mid = middle == 1
+    mid = 1 + t // last
+    end = (t - 1) * last
+    across = last - t
+    far_end_of_end = last - t
+    far_mid_of_end = last - mid
+    far_end_of_mid = (2 - t) * last
+
+    def block(index):
+        return pl.ds(pl.multiple_of(index * rows, rows), rows)
+
+    def chunk(index):
+        return pl.ds(pl.multiple_of(index * width, width), width)
+
+    loads = [
+        pltpu.make_async_copy(src, dst, load_sem.at[i])
+        for i, (src, dst) in enumerate(((k_hbm, k_home), (x_hbm, x_home), (b_hbm, b_home)))
+    ]
+    for load in loads:
+        load.start()
+
+    barrier = pltpu.get_barrier_semaphore()
+    pl.semaphore_signal(barrier, inc=1, device_id=(partner, t), device_id_type=MESH)
+
+    @pl.when(is_end)
+    def _():
+        pl.semaphore_signal(barrier, inc=1, device_id=(g, mid), device_id_type=MESH)
+
+    @pl.when(is_mid)
+    def _():
+        pl.semaphore_signal(barrier, inc=1, device_id=(g, end), device_id_type=MESH)
+        pl.semaphore_signal(barrier, inc=1, device_id=(g, across), device_id_type=MESH)
+
+    def find(wanted):
+        index, here = jnp.int32(0), jnp.int32(0)
+        for j in range(home):
+            hit = plan[g * home + j] == wanted
+            index, here = jnp.where(hit, j, index), jnp.where(hit, 1, here)
+        return index, here > 0
+
+    mine = [find(g * OWN + s) for s in range(OWN)]
+    theirs = [find(partner * OWN + s) for s in range(OWN)]
+
+    def migrate(s, kind):
+        src, dst = ((k_out, k_in), (x_out, x_in), (b_out, b_in))[kind]
+        return pltpu.make_async_remote_copy(
+            src_ref=src.at[s], dst_ref=dst.at[s], send_sem=mig_send.at[s, kind], recv_sem=mig_recv.at[s, kind],
+            device_id=(partner, t), device_id_type=MESH,
+        )
+
+    def gather(src, dst, count):
+        for s in range(OWN):
+            @pl.loop(0, count // STRIP)
+            def _(i):
+                at = pl.ds(pl.multiple_of(i * STRIP, STRIP), STRIP)
+                dst[s, at, :] = src[theirs[s][0], at, :]
+
+    loads[0].wait()
+    gather(k_home, k_out, depth)
+    loads[1].wait()
+    gather(x_home, x_out, depth)
+
+    @pl.when(is_end)
+    def _():
+        pl.semaphore_wait(barrier, 2)
+
+    @pl.when(is_mid)
+    def _():
+        pl.semaphore_wait(barrier, 3)
+
+    for s in range(OWN):
+        for kind in range(2):
+            migrate(s, kind).start()
+
+    def settle(s):
+        migrate(s, 0).wait_recv()
+        migrate(s, 1).wait_recv()
+        index, here = mine[s]
+
+        @pl.loop(0, depth // STRIP)
+        def _(i):
+            at = pl.ds(pl.multiple_of(i * STRIP, STRIP), STRIP)
+            k_got[s, at, :] = jnp.where(here, k_home[index, at, :], k_in[s, at, :])
+            x_got[s, at, :] = jnp.where(here, x_home[index, at, :], x_in[s, at, :])
+
+    def stack_own(s):
+        @pl.loop(0, depth // STRIP)
+        def _(i):
+            first = pl.multiple_of(i * STRIP, STRIP)
+            at = pl.ds(first, STRIP)
+            everything = slice(None)
+            split_into(k_stack, s, 0, depth, first, everything, k_got[s, at, :], (0, 0, 1))
+            split_into(x_stack, s, 0, depth, first, everything, x_got[s, at, :], (0, 1, 0))
+
+    def send_stiffness():
+        loads[2].wait()
+        gather(b_home, b_out, rows)
+        for s in range(OWN):
+            migrate(s, 2).start()
+
+    def stiffness(s, c):
+        index, here = mine[s]
+        return jnp.where(here, b_home[index, :, chunk(c)], b_in[s, :, chunk(c)])
+
+    def feed_k(s, j):
+        target = (far_end_of_end, far_mid_of_end, mid)[j]
+        return pltpu.make_async_remote_copy(
+            src_ref=k_got.at[s, :, block(target)], dst_ref=k_end.at[s, j],
+            send_sem=em_send.at[s, j], recv_sem=em_recv.at[s, j], device_id=(g, mid), device_id_type=MESH,
+        )
+
+    def feed_x(s, c):
+        return pltpu.make_async_remote_copy(
+            src_ref=x_got.at[s, :, chunk(c)], dst_ref=x_end.at[s, :, chunk(c)],
+            send_sem=em_send.at[s, last + c], recv_sem=em_recv.at[s, last + c],
+            device_id=(g, mid), device_id_type=MESH,
+        )
+
+    def cross(s, j, c):
+        return pltpu.make_async_remote_copy(
+            src_ref=p_send.at[s, j, c], dst_ref=p_recv.at[s, j, c],
+            send_sem=mm_send.at[s, j, c], recv_sem=mm_recv.at[s, j, c],
+            device_id=(g, across), device_id_type=MESH,
+        )
+
+    def deliver(s, c):
+        return pltpu.make_async_remote_copy(
+            src_ref=e_send.at[s, c], dst_ref=e_recv.at[s, c],
+            send_sem=me_send.at[s, c], recv_sem=me_recv.at[s, c],
+            device_id=(g, end), device_id_type=MESH,
+        )
+
+    def write(s, c):
+        return pltpu.make_async_copy(
+            result.at[s, :, chunk(c)], out_hbm.at[s, :, chunk(c)], out_sem.at[s, c]
+        )
+
+    own_terms = pl.ds(0, 3 * depth)
+
+    @pl.when(is_end)
+    def _():
+        for s in range(OWN):
+            settle(s)
+            feed_k(s, 0).start()
+            for c in range(CHUNKS):
+                feed_x(s, c).start()
+            feed_k(s, 1).start()
+            feed_k(s, 2).start()
+        send_stiffness()
+        for s in range(OWN):
+            stack_own(s)
+        for s in range(OWN):
+            migrate(s, 2).wait_recv()
+
+            @pl.loop(0, CHUNKS)
+            def _(c):
+                result[s, :, chunk(c)] = stiffness(s, c) - contract(
+                    k_stack[s, own_terms, block(t)], x_stack[s, own_terms, chunk(c)]
+                )
+
+        for s in range(OWN):
+            @pl.loop(0, CHUNKS)
+            def _(c):
+                pltpu.make_async_remote_copy(
+                    src_ref=e_send.at[s, c], dst_ref=e_recv.at[s, c],
+                    send_sem=me_send.at[s, c], recv_sem=me_recv.at[s, c],
+                    device_id=(g, mid), device_id_type=MESH,
+                ).wait_recv()
+                result[s, :, chunk(c)] = result[s, :, chunk(c)] - e_recv[s, c]
+                write(s, c).start()
+
+        for s in range(OWN):
+            for j in range(last):
+                feed_k(s, j).wait_send()
+            for c in range(CHUNKS):
+                feed_x(s, c).wait_send()
+
+    @pl.when(is_mid)
+    def _():
+        def arrive_k(s, j, target):
+            pltpu.make_async_remote_copy(
+                src_ref=k_end.at[s, j], dst_ref=k_end.at[s, j],
+                send_sem=em_send.at[s, j], recv_sem=em_recv.at[s, j], device_id=(g, end), device_id_type=MESH,
+            ).wait_recv()
+
+            @pl.loop(0, depth // STRIP)
+            def _(i):
+                first = pl.multiple_of(i * STRIP, STRIP)
+                split_into(
+                    k_stack, s, 3 * depth, depth, first, block(target), k_end[s, j, pl.ds(first, STRIP), :], (0, 0, 1)
+                )
+
+        def arrive_x(s, c):
+            pltpu.make_async_remote_copy(
+                src_ref=x_end.at[s, :, chunk(c)], dst_ref=x_end.at[s, :, chunk(c)],
+                send_sem=em_send.at[s, last + c], recv_sem=em_recv.at[s, last + c],
+                device_id=(g, end), device_id_type=MESH,
+            ).wait_recv()
+
+            @pl.loop(0, depth // STRIP)
+            def _(i):
+                first = pl.multiple_of(i * STRIP, STRIP)
+                split_into(
+                    x_stack, s, 3 * depth, depth, first, chunk(c), x_end[s, pl.ds(first, STRIP), chunk(c)], (0, 1, 0)
+                )
+
+        def produce(s):
+            arrive_k(s, 0, far_end_of_mid)
+
+            @pl.loop(0, CHUNKS)
+            def _(c):
+                arrive_x(s, c)
+                p_send[s, 0, c] = contract(k_stack[s, :, block(far_end_of_mid)], x_stack[s, :, chunk(c)])
+                cross(s, 0, c).start()
+
+            arrive_k(s, 1, across)
+
+            @pl.loop(0, CHUNKS)
+            def _(c):
+                p_send[s, 1, c] = contract(k_stack[s, :, block(across)], x_stack[s, :, chunk(c)])
+                cross(s, 1, c).start()
+
+        def forward(s):
+            @pl.loop(0, CHUNKS)
+            def _(c):
+                part = contract(k_stack[s, own_terms, block(end)], x_stack[s, own_terms, chunk(c)])
+                cross(s, 0, c).wait_recv()
+                e_send[s, c] = p_recv[s, 0, c] + part
+                deliver(s, c).start()
+
+        def own_share(s):
+            arrive_k(s, 2, t)
+            migrate(s, 2).wait_recv()
+
+            @pl.loop(0, CHUNKS)
+            def _(c):
+                result[s, :, chunk(c)] = stiffness(s, c) - contract(k_stack[s, :, block(t)], x_stack[s, :, chunk(c)])
+
+        def finish(s):
+            @pl.loop(0, CHUNKS)
+            def _(c):
+                cross(s, 1, c).wait_recv()
+                result[s, :, chunk(c)] = result[s, :, chunk(c)] - p_recv[s, 1, c]
+                write(s, c).start()
+
+        for s in range(OWN):
+            settle(s)
+            stack_own(s)
+        produce(0)
+        send_stiffness()
+        forward(0)
+        produce(1)
+        own_share(0)
+        own_share(1)
+        finish(0)
+        forward(1)
+        finish(1)
+        for s in range(OWN):
+            for c in range(CHUNKS):
+                cross(s, 0, c).wait_send()
+                cross(s, 1, c).wait_send()
+                deliver(s, c).wait_send()
+
+    for s in range(OWN):
+        for kind in range(3):
+            migrate(s, kind).wait_send()
+        for c in range(CHUNKS):
+            write(s, c).wait()
+
+
+def line_body(coupling, interior_solve, boundary_stiffness, migration):
+    home, depth, columns = interior_solve.shape
+    rows = boundary_stiffness.shape[1]
+    width = columns // CHUNKS
+    f32, bf16 = jnp.float32, jnp.bfloat16
+    share = (OWN, depth, columns)
+    pieces = (OWN, CHUNKS, rows, width)
+    dma = pltpu.SemaphoreType.DMA
+    return pl.pallas_call(
+        line_kernel,
+        out_shape=jax.ShapeDtypeStruct((OWN, rows, columns), f32),
+        in_specs=[pl.BlockSpec(memory_space=pltpu.SMEM)] + [pl.BlockSpec(memory_space=pl.ANY)] * 3,
+        out_specs=pl.BlockSpec(memory_space=pl.ANY),
+        scratch_shapes=[
+            pltpu.VMEM((home, depth, columns), f32),
+            pltpu.VMEM((home, depth, columns), f32),
+            pltpu.VMEM((home, rows, columns), f32),
+            pltpu.VMEM(share, f32),
+            pltpu.VMEM(share, f32),
+            pltpu.VMEM((OWN, rows, columns), f32),
+            pltpu.VMEM(share, f32),
+            pltpu.VMEM(share, f32),
+            pltpu.VMEM((OWN, rows, columns), f32),
+            pltpu.VMEM(share, f32),
+            pltpu.VMEM(share, f32),
+            pltpu.VMEM((OWN, LINE - 1, depth, rows), f32),
+            pltpu.VMEM(share, f32),
+            pltpu.VMEM((OWN, 6 * depth, columns), bf16),
+            pltpu.VMEM((OWN, 6 * depth, columns), bf16),
+            pltpu.VMEM((OWN, 2, CHUNKS, rows, width), f32),
+            pltpu.VMEM((OWN, 2, CHUNKS, rows, width), f32),
+            pltpu.VMEM(pieces, f32),
+            pltpu.VMEM(pieces, f32),
+            pltpu.VMEM((OWN, rows, columns), f32),
+            dma((3,)),
+            dma((OWN, 3)),
+            dma((OWN, 3)),
+            dma((OWN, LINE - 1 + CHUNKS)),
+            dma((OWN, LINE - 1 + CHUNKS)),
+            dma((OWN, 2, CHUNKS)),
+            dma((OWN, 2, CHUNKS)),
+            dma((OWN, CHUNKS)),
+            dma((OWN, CHUNKS)),
+            dma((OWN, CHUNKS)),
+        ],
+        compiler_params=pltpu.CompilerParams(
+            collective_id=0, has_side_effects=True, vmem_limit_bytes=60 * 1024 * 1024
+        ),
+    )(migration, jnp.swapaxes(coupling, 1, 2), interior_solve, boundary_stiffness)
+
+
 def solution(mesh):
     return jax.shard_map(
-        body,
+        line_body if mesh.shape["tile"] == LINE else portable_body,
         mesh=mesh,
         in_specs=(
             P("group", None, "tile"),

time: 207 us -> 116 us (0.56)
  waiting for transfers between devices: 134 us -> 0 us
  Pallas kernels: 0 us -> 113 us
  other arithmetic: 22.6 us -> 0 us
  local copies, waits for them, and re-layouts: 22.7 us -> 3.16 us
  between operations: 13.5 us -> 0.01 us
  matrix products: 12 us -> 0 us
    reduce_scatter x2 -> x0, waiting for transfers between devices: 134 us -> none  [condense(): lax.psum_scatter(jnp.dot(coupling_cols, solve_rows, precision=lax.Precisi...]
    pallas_call x0 -> x1, Pallas kernels: none -> 113 us  [line_body(): pl.pallas_call(line_kernel, out_shape=jax.ShapeDtypeStruct((OWN, rows, co...]
    gather x6 -> x0, local copies, waits for them, and re-layouts: 20.1 us -> none  [the longest x3 10.3 us: select_slots(): chosen = jnp.take(stacked, positions, axis=0)]
    select_n x8 -> x0, other arithmetic: 18.1 us -> none  [the longest x3 9.14 us: select_slots(): return jnp.where(shaped, chosen, jnp.zeros_like(chosen))]
    dot_general x2 -> x0, matrix products: 12 us -> none  [condense(): jnp.dot(coupling_cols, solve_rows, precision=lax.Precision.HIGHEST, prefe...]
    another operation x2 -> x0, other arithmetic: 4.04 us -> none  [body(): jnp.stack([condense(kept_coupling[slot], kept_solve[slot], kept_stiff[slo...]
  transfers between devices with their start and end apart: 5 -> 0, of which waited for: 3 -> 0; matrix products, arithmetic and copies ran while one was open for 18% -> 0% of each run, Pallas kernels for 0% -> 0%
where the time goes in v1:
time: 116 us
  Pallas kernels  113 us (97%)
  local copies, waits for them, and re-layouts  3.16 us (3%)
    pallas_call x1, Pallas kernels, line_body(): pl.pallas_call(line_kernel, out_shape=jax.ShapeDtypeStruct((OWN, rows, co...  113 us
    unnamed x1, local copies, waits for them, and re-layouts  3.16 us

profile of v1, /device:TPU:8, one launch (start us, length us, event | category | flops | bytes accessed | tf_op | source)
XLA Modules:
  0.0 116.0 jit_solution(239371961014207773)
XLA Ops:
  0.0 112.8 %shard_map.46 = f32[2,256,1024]{2,1,0:T(8,128)} custom-call(s32[32]{0:T(128)} %plan.1, f32[4,192,1024]{2,1,0:T(8,128)} %bitcast.1, f32[4,192,1024]{2,1,0:T(8,128)} %x_hbm.1, f32[4,256,1024]{2,1,0:T(8,128)} %b_hbm.1), custom_call_target="tpu_custom_call" | custom-call | tf_op jit(solution)/shard_map/pallas_call | solution.py:377
  112.8 3.2 %copy.6 = f32[2,256,1024]{2,1,0:T(8,128)} copy(f32[2,256,1024]{2,1,0:T(8,128)} %shard_map.46) | data formatting | bytes 4194304

commit v2 on v1

--- a/solution.py
+++ b/solution.py
@@ -66,7 +66,7 @@
 
 MESH = pl.DeviceIdType.MESH
 LINE = 4
-CHUNKS = 4
+CHUNKS = 8
 STRIP = 16
 
 
@@ -83,10 +83,10 @@
 
 
 def line_kernel(
-    plan, k_hbm, x_hbm, b_hbm, out_hbm,
+    plan, k_hbm, x_hbm, b_hbm, result,
     k_home, x_home, b_home, k_out, x_out, b_out, k_in, x_in, b_in, k_got, x_got,
-    k_end, x_end, k_stack, x_stack, p_send, p_recv, e_send, e_recv, result,
-    load_sem, mig_send, mig_recv, em_send, em_recv, mm_send, mm_recv, me_send, me_recv, out_sem,
+    k_end, x_end, k_stack, x_stack, p_send, p_recv, e_send, e_recv,
+    load_sem, mig_send, mig_recv, em_send, em_recv, mm_send, mm_recv, me_send, me_recv,
 ):
     home, depth, columns = x_home.shape
     rows = b_home.shape[1]
@@ -114,8 +114,8 @@
         pltpu.make_async_copy(src, dst, load_sem.at[i])
         for i, (src, dst) in enumerate(((k_hbm, k_home), (x_hbm, x_home), (b_hbm, b_home)))
     ]
-    for load in loads:
-        load.start()
+    loads[0].start()
+    loads[1].start()
 
     barrier = pltpu.get_barrier_semaphore()
     pl.semaphore_signal(barrier, inc=1, device_id=(partner, t), device_id_type=MESH)
@@ -169,17 +169,17 @@
     for s in range(OWN):
         for kind in range(2):
             migrate(s, kind).start()
-
-    def settle(s):
-        migrate(s, 0).wait_recv()
-        migrate(s, 1).wait_recv()
+    loads[2].start()
+
+    def settle(s, kind):
+        migrate(s, kind).wait_recv()
         index, here = mine[s]
+        got, own, arrived = ((k_got, k_home, k_in), (x_got, x_home, x_in))[kind]
 
         @pl.loop(0, depth // STRIP)
         def _(i):
             at = pl.ds(pl.multiple_of(i * STRIP, STRIP), STRIP)
-            k_got[s, at, :] = jnp.where(here, k_home[index, at, :], k_in[s, at, :])
-            x_got[s, at, :] = jnp.where(here, x_home[index, at, :], x_in[s, at, :])
+            got[s, at, :] = jnp.where(here, own[index, at, :], arrived[s, at, :])
 
     def stack_own(s):
         @pl.loop(0, depth // STRIP)
@@ -228,18 +228,14 @@
             device_id=(g, end), device_id_type=MESH,
         )
 
-    def write(s, c):
-        return pltpu.make_async_copy(
-            result.at[s, :, chunk(c)], out_hbm.at[s, :, chunk(c)], out_sem.at[s, c]
-        )
-
     own_terms = pl.ds(0, 3 * depth)
 
     @pl.when(is_end)
     def _():
         for s in range(OWN):
-            settle(s)
+            settle(s, 0)
             feed_k(s, 0).start()
+            settle(s, 1)
             for c in range(CHUNKS):
                 feed_x(s, c).start()
             feed_k(s, 1).start()
@@ -265,7 +261,6 @@
                     device_id=(g, mid), device_id_type=MESH,
                 ).wait_recv()
                 result[s, :, chunk(c)] = result[s, :, chunk(c)] - e_recv[s, c]
-                write(s, c).start()
 
         for s in range(OWN):
             for j in range(last):
@@ -339,10 +334,10 @@
             def _(c):
                 cross(s, 1, c).wait_recv()
                 result[s, :, chunk(c)] = result[s, :, chunk(c)] - p_recv[s, 1, c]
-                write(s, c).start()
-
-        for s in range(OWN):
-            settle(s)
+
+        for s in range(OWN):
+            settle(s, 0)
+            settle(s, 1)
             stack_own(s)
         produce(0)
         send_stiffness()
@@ -362,8 +357,6 @@
     for s in range(OWN):
         for kind in range(3):
             migrate(s, kind).wait_send()
-        for c in range(CHUNKS):
-            write(s, c).wait()
 
 
 def line_body(coupling, interior_solve, boundary_stiffness, migration):
@@ -376,9 +369,9 @@
     dma = pltpu.SemaphoreType.DMA
     return pl.pallas_call(
         line_kernel,
-        out_shape=jax.ShapeDtypeStruct((OWN, rows, columns), f32),
+        out_shape=pltpu.VMEM((OWN, rows, columns), f32),
         in_specs=[pl.BlockSpec(memory_space=pltpu.SMEM)] + [pl.BlockSpec(memory_space=pl.ANY)] * 3,
-        out_specs=pl.BlockSpec(memory_space=pl.ANY),
+        out_specs=pl.BlockSpec(memory_space=pltpu.VMEM),
         scratch_shapes=[
             pltpu.VMEM((home, depth, columns), f32),
             pltpu.VMEM((home, depth, columns), f32),
@@ -399,7 +392,6 @@
             pltpu.VMEM((OWN, 2, CHUNKS, rows, width), f32),
             pltpu.VMEM(pieces, f32),
             pltpu.VMEM(pieces, f32),
-            pltpu.VMEM((OWN, rows, columns), f32),
             dma((3,)),
             dma((OWN, 3)),
             dma((OWN, 3)),
@@ -407,7 +399,6 @@
             dma((OWN, LINE - 1 + CHUNKS)),
             dma((OWN, 2, CHUNKS)),
             dma((OWN, 2, CHUNKS)),
-            dma((OWN, CHUNKS)),
             dma((OWN, CHUNKS)),
             dma((OWN, CHUNKS)),
         ],

time: 116 us -> 111 us (0.957)
  Pallas kernels: 113 us -> 109 us
  local copies, waits for them, and re-layouts: 3.16 us -> 1.32 us
    pallas_call x1, Pallas kernels: 113 us -> 109 us  [line_body(): pl.pallas_call(line_kernel, out_shape=pltpu.VMEM((OWN, rows, columns), f3...]
    unnamed x1, local copies, waits for them, and re-layouts: 3.16 us -> 1.32 us
where the time goes in v2:
time: 111 us
  Pallas kernels  109 us (98%)
  local copies, waits for them, and re-layouts  1.32 us (1%)
    pallas_call x1, Pallas kernels, line_body(): pl.pallas_call(line_kernel, out_shape=pltpu.VMEM((OWN, rows, columns), f3...  109 us

profile of v2, /device:TPU:8, one launch (start us, length us, event | category | flops | bytes accessed | tf_op | source)
XLA Modules:
  0.0 110.6 jit_solution(7177657385221884131)
XLA Ops:
  0.0 109.2 %shard_map.46 = f32[2,256,1024]{2,1,0:T(8,128)S(1)} custom-call(s32[32]{0:T(128)} %plan.1, f32[4,192,1024]{2,1,0:T(8,128)} %bitcast.1, f32[4,192,1024]{2,1,0:T(8,128)} %x_hbm.1, f32[4,256,1024]{2,1,0:T(8,128)} %b_hbm.1), custom_call_target="tpu_custom_call" | custom-call | tf_op jit(solution)/shard_map/pallas_call | solution.py:370
  109.3 1.3 %copy.6 = f32[2,256,1024]{2,1,0:T(8,128)} copy(f32[2,256,1024]{2,1,0:T(8,128)S(1)} %shard_map.46) | data formatting | bytes 4194304
